TPU v7x, 32 devices: a 4x2x2 block of a 4x4x8 slice. The times are simulated.
32 devices in a mesh: dp: 4 (over y, z), tp: 8 (over x, core).
Axes of the slice: x: 4, y: 2, z: 2, core: 2. Of those that a mesh axis runs over, the one named last changes fastest.
The devices are a block of a 4x4x8 slice.
Arguments:
- x_chunk: bfloat16 [16, 1024, 2048], P('dp', 'tp'), parts along dimension 0
- prefix_len: int32 [16], P('dp'), parts along dimension 0
- k_cache: bfloat16 [16, 4096, 16, 128], P('dp', None, 'tp'), parts along dimension 0
- v_cache: bfloat16 [16, 4096, 16, 128], P('dp', None, 'tp'), parts along dimension 0
- ln1_gain: bfloat16 [2048], replicated
- ln1_bias: bfloat16 [2048], replicated
- w_qkv: bfloat16 [2048, 6144], P(None, 'tp')
- b_qkv: bfloat16 [6144], P('tp')
- w_out: bfloat16 [2048, 2048], P('tp')
- b_out: bfloat16 [2048], replicated
- ln2_gain: bfloat16 [2048], replicated
- ln2_bias: bfloat16 [2048], replicated
- w_up: bfloat16 [2048, 8192], P(None, 'tp')
- b_up: bfloat16 [8192], P('tp')
- w_down: bfloat16 [8192, 2048], P('tp')
- b_down: bfloat16 [2048], replicated
Outputs:
- output 1: bfloat16 [16, 1024, 2048], P('dp', 'tp'), parts along dimension 0
- output 2: bfloat16 [16, 4096, 16, 128], P('dp', None, 'tp'), parts along dimension 0
- output 3: bfloat16 [16, 4096, 16, 128], P('dp', None, 'tp'), parts along dimension 0
There are 4 independent parts. A program takes and returns all parts, laid end to end along the dimension named above; an argument that names none is the same for every part.
All inputs are finite; a program needn't handle non-finite values.
Results may differ from a plain program's by a relative error of at most 0.0132017.
Values are sent between devices in bfloat16 or wider.
A program may use at most 768 MiB of HBM per device.

v0:
```python
import jax
import jax.numpy as jnp
from jax import lax
from jax.sharding import PartitionSpec as P

LN_EPS = 1e-5


def layer_norm(tok_rows, ln_gain, ln_bias):
    rows_f32 = tok_rows.astype(jnp.float32)
    row_mean = jnp.mean(rows_f32, axis=-1, keepdims=True)
    centered = rows_f32 - row_mean
    row_var = jnp.mean(centered * centered, axis=-1, keepdims=True)
    normed = centered * lax.rsqrt(row_var + LN_EPS)
    return (normed * ln_gain.astype(jnp.float32) + ln_bias.astype(jnp.float32)).astype(jnp.bfloat16)


def write_rows(cache_seq, new_rows, start_pos):
    zero_idx = jnp.zeros_like(start_pos)
    return lax.dynamic_update_slice(cache_seq, new_rows, (start_pos, zero_idx, zero_idx))


def attend(queries, k_upd, v_upd, prefix_len, head_offset, heads_all):
    batch_n, chunk_len, heads_loc, head_dim = queries.shape
    cache_len = k_upd.shape[1]
    scores = jnp.einsum('bchd,bthd->bhct', queries, k_upd, preferred_element_type=jnp.float32) * (head_dim ** -0.5)
    head_ids = head_offset + jnp.arange(heads_loc)
    slopes = jnp.exp2(-8.0 * (head_ids + 1).astype(jnp.float32) / heads_all)
    query_pos = prefix_len[:, None] + jnp.arange(chunk_len)[None, :]
    rel_pos = (jnp.arange(cache_len)[None, None, :] - query_pos[:, :, None]).astype(jnp.float32)
    scores = scores + slopes[None, :, None, None] * rel_pos[:, None]
    scores = jnp.where((rel_pos <= 0.0)[:, None], scores, -1e30)
    attn_probs = jax.nn.softmax(scores, axis=-1).astype(jnp.bfloat16)
    context = jnp.einsum('bhct,bthd->bchd', attn_probs, v_upd, preferred_element_type=jnp.float32)
    return context.astype(jnp.bfloat16).reshape(batch_n, chunk_len, heads_loc * head_dim)


def solution(mesh):
    tp_size = mesh.shape['tp']

    def local_layer(x_local, prefix_len, k_cache, v_cache, ln1_gain, ln1_bias, w_qkv, b_qkv, w_out, b_out, ln2_gain, ln2_bias, w_up, b_up, w_down, b_down):
        batch_n, tok_loc = x_local.shape[0], x_local.shape[1]
        heads_loc, head_dim = k_cache.shape[2], k_cache.shape[3]
        chunk_len = tok_loc * tp_size
        normed = layer_norm(x_local, ln1_gain, ln1_bias)
        gathered = lax.all_gather(normed, 'tp', axis=1, tiled=True)
        qkv_proj = jnp.einsum('bcd,de->bce', gathered, w_qkv, preferred_element_type=jnp.float32) + b_qkv.astype(jnp.float32)
        qkv_heads = qkv_proj.astype(jnp.bfloat16).reshape(batch_n, chunk_len, heads_loc, 3, head_dim)
        k_upd = jax.vmap(write_rows)(k_cache, qkv_heads[:, :, :, 1], prefix_len)
        v_upd = jax.vmap(write_rows)(v_cache, qkv_heads[:, :, :, 2], prefix_len)
        head_offset = lax.axis_index('tp') * heads_loc
        context = attend(qkv_heads[:, :, :, 0], k_upd, v_upd, prefix_len, head_offset, heads_loc * tp_size)
        attn_part = jnp.einsum('bce,ed->bcd', context, w_out, preferred_element_type=jnp.float32).astype(jnp.bfloat16)
        attn_sum = lax.psum_scatter(attn_part, 'tp', scatter_dimension=1, tiled=True)
        residual = (x_local.astype(jnp.float32) + attn_sum.astype(jnp.float32) + b_out.astype(jnp.float32)).astype(jnp.bfloat16)
        normed2 = layer_norm(residual, ln2_gain, ln2_bias)
        gathered2 = lax.all_gather(normed2, 'tp', axis=1, tiled=True)
        up_pre = jnp.einsum('bcd,df->bcf', gathered2, w_up, preferred_element_type=jnp.float32) + b_up.astype(jnp.float32)
        up_act = jax.nn.gelu(up_pre, approximate=True).astype(jnp.bfloat16)
        down_part = jnp.einsum('bcf,fd->bcd', up_act, w_down, preferred_element_type=jnp.float32).astype(jnp.bfloat16)
        down_sum = lax.psum_scatter(down_part, 'tp', scatter_dimension=1, tiled=True)
        x_out = (residual.astype(jnp.float32) + down_sum.astype(jnp.float32) + b_down.astype(jnp.float32)).astype(jnp.bfloat16)
        return x_out, k_upd, v_upd

    tok_spec = P('dp', 'tp', None)
    cache_spec = P('dp', None, 'tp', None)
    replicated = P()
    in_specs = (tok_spec, P('dp'), cache_spec, cache_spec, replicated, replicated, P(None, 'tp'), P('tp'), P('tp', None), replicated, replicated, replicated, P(None, 'tp'), P('tp'), P('tp', None), replicated)
    return jax.shard_map(local_layer, mesh=mesh, in_specs=in_specs, out_specs=(tok_spec, cache_spec, cache_spec), check_vma=False)
```

profile of v0, /device:TPU:81, one launch (start us, length us, event | category | flops | bytes accessed | tf_op | source)
XLA Modules:
  0.0 690.5 jit_solution(9448666428085057154)
XLA Ops:
  7.3 8.2 %copy.66 = bf16[4,4096,2,128]{3,2,1,0:T(2,128)(2,1)} copy(bf16[4,4096,2,128]{3,2,1,0:T(2,128)(2,1)} %param.18) | data formatting | bytes 16777216
  23.7 21.3 %subtract_convert_fusion = f32[4,1024,4096]{2,1,0:T(8,128)} fusion(s32[4,1024]{1,0:T(4,128)S(1)} %iota_add_fusion), kind=kLoop, calls=%fused_computation.17 | loop fusion | flops 33554432 | bytes 67125248 | tf_op jit(solution)/shard_map/convert_element_type | solution.py:30
  45.0 15.5 %broadcast_compare_fusion = pred[4,1024,4096]{2,1,0:T(8,128)(4,1)} fusion(s32[4,1024]{1,0:T(4,128)S(1)} %iota_add_fusion), kind=kLoop, calls=%fused_computation.20 | loop fusion | flops 50331648 | bytes 16793600 | tf_op jit(solution)/shard_map/le | solution.py:32
  60.5 49.4 %all-gather.3.cloned.1.call-done = bf16[4,1024,2048]{2,1,0:T(8,128)(2,1)} async-done(((bf16[4,128,2048]{2,1,0:T(8,128)(2,1)}), bf16[4,1024,2048]{2,1,0:T(8,128)(2,1)}) %all-gather.3.cloned.1.call-update) | async-done | bytes 16777232 | tf_op jit(solution)/shard_map/all_gather | solution.py:46
  109.9 18.8 %add_convert_fusion = bf16[4,1024,768]{1,2,0:T(8,128)(2,1)} fusion(f32[768]{0:T(1024)S(1)} %convert_element_type.92, bf16[4,1024,2048]{2,1,0:T(8,128)(2,1)} %all-gather.3.cloned.1.call-done, bf16[2048,768]{1,0:T(8,128)(2,1)S(1)} %copy-done), kind=kOutput, calls=%fused_computation.33 | convolution fusion | flops 12891193344 | bytes 26217472 | tf_op jit(solution)/shard_map/bcd,de->bce/dot_general | solution.py:47
  128.7 4.9 fusion.57
  133.6 4.7 copy.33
  138.3 33.0 %while.3 = (s32[]{:T(128)}, bf16[4,4096,2,128]{3,2,1,0:T(2,128)(2,1)}, s32[4,4]{1,0:T(4,128)S(1)}, bf16[4,1024,2,128]{3,2,1,0:T(2,128)(2,1)S(1)}, s32[]{:T(128)}, /*index=5*/s32[4]{0:T(128)S(1)}) while((s32[]{:T(128)}, bf16[4,4096,2,128]{3,2,1,0:T(2,128)(2,1)}, s32[4,4]{1,0:T(4,128)S(1)}, bf16[4,1024,2,128]{3,2,1,0:T(2,128)(2,1)S(1)}, s32[]{:T(128)}, ...), condition=%wide.while_cond.1, body=%wide.while_body.1.sunk | while | flops 262173 | bytes 1575082 | solution.py:20
  158.7 4.3 fusion.74
  171.3 4.7 copy.31
  176.0 33.3 %while.2 = (s32[]{:T(128)}, bf16[4,4096,2,128]{3,2,1,0:T(2,128)(2,1)}, s32[4,4]{1,0:T(4,128)S(1)}, bf16[4,1024,2,128]{3,2,1,0:T(2,128)(2,1)S(1)}, s32[]{:T(128)}, /*index=5*/s32[4]{0:T(128)S(1)}) while((s32[]{:T(128)}, bf16[4,4096,2,128]{3,2,1,0:T(2,128)(2,1)}, s32[4,4]{1,0:T(4,128)S(1)}, bf16[4,1024,2,128]{3,2,1,0:T(2,128)(2,1)S(1)}, s32[]{:T(128)}, ...), condition=%wide.while_cond, body=%wide.while_body.sunk | while | flops 262173 | bytes 1575082 | solution.py:20
  180.0 4.3 fusion.72
  188.4 4.3 fusion.72
  196.7 4.3 fusion.72
  205.0 4.3 fusion.72
  209.3 104.8 %fusion.58 = (f32[4,2,1024]{2,1,0:T(2,128)S(1)}, f32[4,2,1024,4096]{3,2,1,0:T(8,128)}) fusion(f32[4,1024,4096]{2,1,0:T(8,128)} %subtract_convert_fusion, f32[2]{0:T(128)S(1)} %multiply_exponential_fusion, pred[4,1024,4096]{2,1,0:T(8,128)(4,1)} %broadcast_compare_fusion, bf16[4,4096,2,128]{3,2,1,0:T(2,128)(2,1)} %get-tuple-element.16, ...), kind=kOutput, calls=%fused_computation.81 | convolution fusion | flops 8791265280 | bytes 228622336 | tf_op jit(solution)/shard_map/sub | solution.py:33
  314.1 45.6 %fusion.47 = bf16[4,2,128,1024]{3,2,1,0:T(8,128)(2,1)S(1)} fusion(f32[4,2,1024,4096]{3,2,1,0:T(8,128)} %get-tuple-element.56, f32[4,2,1024]{2,1,0:T(2,128)S(1)} %get-tuple-element.55, bf16[4,4096,2,128]{3,2,1,0:T(2,128)(2,1)} %get-tuple-element.8), kind=kOutput, calls=%fused_computation.64 | convolution fusion | flops 8658092032 | bytes 144736256 | tf_op jit(solution)/shard_map/bhct,bthd->bchd/dot_general | solution.py:34
  359.7 8.1 %convolution_convert_fusion.1 = bf16[4,1024,2048]{2,1,0:T(8,128)(2,1)} fusion(bf16[4,1024,256]{1,2,0:T(8,128)(2,1)S(1)} %bitcast.73, bf16[256,2048]{1,0:T(8,128)(2,1)S(1)} %copy-done.6), kind=kOutput, calls=%fused_computation.32 | convolution fusion | flops 4303355904 | bytes 19922944 | tf_op jit(solution)/shard_map/bce,ed->bcd/dot_general | solution.py:53
  368.5 87.9 %reduce-scatter.3.cloned.1.call-done = bf16[4,128,2048]{2,1,0:T(8,128)(2,1)} async-done(((bf16[4,1024,2048]{2,1,0:T(8,128)(2,1)}), bf16[4,128,2048]{2,1,0:T(8,128)(2,1)}) %reduce-scatter.3.cloned.1.call-update) | async-done | bytes 2097168 | tf_op jit(solution)/shard_map/reduce_scatter | solution.py:54
  462.7 82.6 %all-gather.5.cloned.1.call-done = bf16[4,1024,2048]{2,1,0:T(8,128)(2,1)} async-done(((bf16[4,128,2048]{2,1,0:T(8,128)(2,1)}), bf16[4,1024,2048]{2,1,0:T(8,128)(2,1)}) %all-gather.5.cloned.1.call-update) | async-done | bytes 16777232 | tf_op jit(solution)/shard_map/all_gather | solution.py:57
  545.3 24.9 %fusion.17 = bf16[4,1024,1024]{2,1,0:T(8,128)(2,1)S(1)} fusion(bf16[4,1024,2048]{2,1,0:T(8,128)(2,1)} %all-gather.5.cloned.1.call-done, f32[1024]{0:T(1024)S(1)} %convert_element_type.107, bf16[2048,1024]{1,0:T(8,128)(2,1)} %param.28), kind=kOutput, calls=%fused_computation.29 | convolution fusion | flops 17221812224 | bytes 29364224 | tf_op jit(solution)/shard_map/bcd,df->bcf/dot_general | solution.py:58
  570.2 20.6 %convolution_convert_fusion = bf16[4,1024,2048]{2,1,0:T(8,128)(2,1)} fusion(bf16[4,1024,1024]{2,1,0:T(8,128)(2,1)S(1)} %fusion.17, bf16[1024,2048]{1,0:T(8,128)(2,1)S(1)} %copy-done.18), kind=kOutput, calls=%fused_computation.31 | convolution fusion | flops 17188257792 | bytes 29360128 | tf_op jit(solution)/shard_map/bcf,fd->bcd/dot_general | solution.py:60
  591.6 87.8 %reduce-scatter.5.cloned.1.call-done = bf16[4,128,2048]{2,1,0:T(8,128)(2,1)} async-done(((bf16[4,1024,2048]{2,1,0:T(8,128)(2,1)}), bf16[4,128,2048]{2,1,0:T(8,128)(2,1)}) %reduce-scatter.5.cloned.1.call-update) | async-done | bytes 2097168 | tf_op jit(solution)/shard_map/reduce_scatter | solution.py:61
  679.4 4.5 fusion.43
  (99 shorter events, 60.6 us)
Async XLA Ops:
  7.2 102.7 %copy-start = (bf16[2048,768]{1,0:T(8,128)(2,1)S(1)}, bf16[2048,768]{1,0:T(8,128)(2,1)}, u32[]{:S(2)}) copy-start(bf16[2048,768]{1,0:T(8,128)(2,1)} %param.22) | copy-start | bytes 9437188
  7.2 102.7 %all-gather.3.cloned.1.call-start = ((), (), s32[]{:S(2)}) async-start(), calls=%async_computation.2 | async-start | bytes 18874368 | tf_op jit(solution)/shard_map/all_gather | solution.py:46
  7.3 9.0 %copy-start.5 = (bf16[4,4096,2,128]{3,2,1,0:T(2,128)(2,1)S(1)}, bf16[4,4096,2,128]{3,2,1,0:T(2,128)(2,1)}, u32[]{:S(2)}) copy-start(bf16[4,4096,2,128]{3,2,1,0:T(2,128)(2,1)} %param.19) | copy-start | bytes 25165828
  16.2 3.6 copy-start.2
  16.2 4.6 copy-start.8
  16.2 4.7 copy-start.9
  19.8 3.6 copy-start.14
  19.8 3.6 copy-start.16
  19.8 3.6 copy-start.17
  23.1 433.3 %reduce-scatter.3.cloned.1.call-start = ((), (), s32[]{:S(2)}) async-start(), calls=%async_computation.3 | async-start | bytes 18874368 | tf_op jit(solution)/shard_map/reduce_scatter | solution.py:54
  128.7 9.6 %copy-start.7 = (s32[4]{0:T(128)S(1)}, s32[4]{0:T(128)}, u32[]{:S(2)}) copy-start(s32[4]{0:T(128)} %constant.142) | copy-start | bytes 52
  314.1 45.6 %copy-start.6 = (bf16[256,2048]{1,0:T(8,128)(2,1)S(1)}, bf16[256,2048]{1,0:T(8,128)(2,1)}, u32[]{:S(2)}) copy-start(bf16[256,2048]{1,0:T(8,128)(2,1)} %param.24) | copy-start | bytes 3145732
  367.8 0.7 copy-start.10
  367.8 0.7 copy-start.11
  367.8 0.7 copy-start.12
  367.8 88.6 %copy-start.3 = (bf16[4,128,2048]{2,1,0:T(8,128)(2,1)S(1)}, bf16[4,128,2048]{2,1,0:T(8,128)(2,1)}, u32[]{:S(2)}) copy-start(bf16[4,128,2048]{2,1,0:T(8,128)(2,1)} %param.16) | copy-start | bytes 6291460
  367.9 94.8 %copy-start.15 = (bf16[1024]{0:T(1024)(128)(2,1)S(1)}, bf16[1024]{0:T(1024)(128)(2,1)}, u32[]{:S(2)}) copy-start(bf16[1024]{0:T(1024)(128)(2,1)} %param.29) | copy-start | bytes 6148
  367.9 177.4 %all-gather.5.cloned.1.call-start = ((), (), s32[]{:S(2)}) async-start(), calls=%async_computation.4 | async-start | bytes 18874368 | tf_op jit(solution)/shard_map/all_gather | solution.py:57
  459.0 1.3 copy-start.4
  462.6 216.8 %reduce-scatter.5.cloned.1.call-start = ((), (), s32[]{:S(2)}) async-start(), calls=%async_computation.5 | async-start | bytes 18874368 | tf_op jit(solution)/shard_map/reduce_scatter | solution.py:61
  545.3 24.9 %copy-start.18 = (bf16[1024,2048]{1,0:T(8,128)(2,1)S(1)}, bf16[1024,2048]{1,0:T(8,128)(2,1)}, u32[]{:S(2)}) copy-start(bf16[1024,2048]{1,0:T(8,128)(2,1)} %param.30) | copy-start | bytes 12582916
  590.8 93.1 %copy-start.1 = (bf16[2048,768]{1,0:T(8,128)(2,1)S(1)}, bf16[2048,768]{1,0:T(8,128)(2,1)}, u32[]{:S(2)}) copy-start(bf16[2048,768]{1,0:T(8,128)(2,1)} %param.22) | copy-start | bytes 9437188
  590.8 0.8 copy-start.13
Sparse Core Ops, SparseCore 0:
  23.2 86.6 all-gather.2
  368.0 88.4 reduce-scatter.2
  462.7 82.5 all-gather.4
  591.0 88.4 reduce-scatter.4
where the time goes:
time: 692 us; the launch traced here: 690 us
  waiting for transfers between devices  308 us (45%)
  matrix products  223 us (32%)
  other arithmetic  111 us (16%)
  local copies, waits for them, and re-layouts  34.3 us (5%)
  between operations  14 us (2%)
    sub x1, matrix products, attend(): attn_probs = jax.nn.softmax(scores, axis=-1).astype(jnp.bfloat16)  105 us
    reduce_scatter x1, waiting for transfers between devices, local_layer(): lax.psum_scatter(attn_part, 'tp', scatter_dimension=1, tiled=True)  87.9 us
    reduce_scatter x1, waiting for transfers between devices, local_layer(): lax.psum_scatter(down_part, 'tp', scatter_dimension=1, tiled=True)  87.8 us
    all_gather x1, waiting for transfers between devices, local_layer(): gathered2 = lax.all_gather(normed2, 'tp', axis=1, tiled=True)  82.6 us
    scatter x16, other arithmetic  60.9 us
    all_gather x1, waiting for transfers between devices, local_layer(): gathered = lax.all_gather(normed, 'tp', axis=1, tiled=True)  49.4 us
    dot_general x1, matrix products, attend(): jnp.einsum('bhct,bthd->bchd', attn_probs, v_upd, preferred_element_type=j...  45.6 us
    dot_general x1, matrix products, local_layer(): jnp.einsum('bcd,df->bcf', gathered2, w_up, preferred_element_type=jnp.flo...  24.9 us
  transfers between devices with their start and end apart: 4, of which 4 were waited for; matrix products, arithmetic and copies ran while one was open for 5% of the time, Pallas kernels for 0%

commit v1 on v0

v1 whole, which is shorter than its diff:
```python
import functools
import math

import jax
import jax.numpy as jnp
from jax import lax
from jax.experimental import pallas as pl
from jax.experimental.pallas import tpu as pltpu
from jax.sharding import PartitionSpec as P


LN_EPS = 1e-5
LOG2E = math.log2(math.e)
NEG = -1e30


def layer_norm(tok_rows, ln_gain, ln_bias):
    rows_f32 = tok_rows.astype(jnp.float32)
    row_mean = jnp.mean(rows_f32, axis=-1, keepdims=True)
    centered = rows_f32 - row_mean
    row_var = jnp.mean(centered * centered, axis=-1, keepdims=True)
    normed = centered * lax.rsqrt(row_var + LN_EPS)
    return (normed * ln_gain.astype(jnp.float32) + ln_bias.astype(jnp.float32)).astype(jnp.bfloat16)


def attn_kernel(seq, q_blk, k_blk, prefix_ref, slope_ref, qkv_ref, k_ref, v_ref, *rest):
    out_ref, knew_ref, vnew_ref, acc_ref, m_ref = rest[-5:]
    head = pl.program_id(0)
    chunk = qkv_ref.shape[0]
    dim = k_ref.shape[3]
    heads = qkv_ref.shape[1] // (3 * dim)
    start = prefix_ref[seq]
    slope = slope_ref[head] * LOG2E
    scale = dim ** -0.5 * LOG2E

    def ones(n):
        return (lax.broadcasted_iota(jnp.int32, (n, dim), 1) == 0).astype(jnp.bfloat16)

    def cols(which):
        return pl.ds(pl.multiple_of((3 * head + which) * dim, dim), dim)

    @pl.when(head == 0)
    def _():
        n = 256
        row = lax.broadcasted_iota(jnp.int32, (n, n), 0)
        pick = (row // heads + row % heads * (n // heads) == lax.broadcasted_iota(jnp.int32, (n, n), 1)).astype(jnp.bfloat16)
        for which, dst in ((1, knew_ref), (2, vnew_ref)):
            for i in range(heads * chunk // n):
                rows = pl.ds(i * (n // heads), n // heads)
                both = jnp.concatenate([qkv_ref[rows, (3 * h + which) * dim:(3 * h + which + 1) * dim] for h in range(heads)], axis=0)
                dst[pl.ds(i * n, n), :] = jnp.dot(pick, both, preferred_element_type=jnp.float32).astype(dst.dtype)

    def update(rows, keys, values, bias, masked=None):
        s = lax.dot_general(qkv_ref[rows, cols(0)], keys, (((1,), (1,)), ((), ())), preferred_element_type=jnp.float32)
        s = s * scale + bias
        if masked is not None:
            s = jnp.where(masked, NEG, s)
        m_old = m_ref[rows, :1]
        m_new = jnp.maximum(m_old, jnp.max(s, axis=1, keepdims=True))
        p = jnp.exp2(s - m_new).astype(jnp.bfloat16)
        pv = lax.dot_general(p, jnp.concatenate([values, ones(values.shape[0])], axis=1), (((1,), (0,)), ((), ())), preferred_element_type=jnp.float32)
        acc_ref[rows, :] = acc_ref[rows, :] * jnp.exp2(m_old - m_new) + pv
        m_ref[rows, :] = jnp.broadcast_to(m_new, (q_blk, m_ref.shape[1]))

    col = lax.broadcasted_iota(jnp.int32, (1, k_blk), 1)
    acc_ref[...] = jnp.zeros_like(acc_ref)
    m_ref[...] = jnp.full_like(m_ref, NEG)
    full = start // k_blk

    def prefix_block(i, masked):
        off = pl.multiple_of(i * k_blk, k_blk)
        keys = k_ref[0, 0, pl.ds(off, k_blk), :]
        values = v_ref[0, 0, pl.ds(off, k_blk), :]
        rel = (off + col - start).astype(jnp.float32)
        for r in range(chunk // q_blk):
            update(pl.ds(r * q_blk, q_blk), keys, values, slope * (rel - float(r * q_blk)), (off + col >= start) if masked else None)

    @pl.loop(0, full)
    def _(i):
        prefix_block(i, False)

    @pl.when(full * k_blk < start)
    def _():
        prefix_block(full, True)

    for r in range(chunk // q_blk):
        n = (r + 1) * q_blk
        new_col = lax.broadcasted_iota(jnp.int32, (1, n), 1) - r * q_blk
        bias = slope * new_col.astype(jnp.float32)
        masked = (lax.broadcasted_iota(jnp.int32, (q_blk, n), 1) - r * q_blk) > lax.broadcasted_iota(jnp.int32, (q_blk, n), 0)
        update(pl.ds(r * q_blk, q_blk), qkv_ref[pl.ds(0, n), cols(1)], qkv_ref[pl.ds(0, n), cols(2)], bias, masked)
    total = acc_ref[:, dim:dim + 1]
    out_ref[:, 0] = (acc_ref[:, :dim] / total).astype(out_ref.dtype).reshape(out_ref.shape[0], out_ref.shape[2], dim)


def attend(seq, prefix_len, slopes, qkv, k_heads, v_heads, owners=8, slots=1, slot=0, buffer=None, q_blk=256, k_blk=1024):
    chunk = qkv.shape[0]
    heads, cache_len, dim = k_heads.shape[1:]
    cache_spec = pl.BlockSpec((1, 1, cache_len, dim), lambda h, *_: (seq, h, 0, 0))
    whole = lambda shape: pl.BlockSpec(shape, lambda h, *_: (0, 0))
    rows = jax.ShapeDtypeStruct((heads * chunk, dim), jnp.bfloat16)
    extra = () if buffer is None else (buffer,)
    return pl.pallas_call(
        functools.partial(attn_kernel, seq, q_blk, k_blk),
        out_shape=(jax.ShapeDtypeStruct((owners, slots, chunk // owners, heads * dim), jnp.bfloat16), rows, rows),
        grid_spec=pltpu.PrefetchScalarGridSpec(
            num_scalar_prefetch=2,
            grid=(heads,),
            in_specs=[whole(qkv.shape), cache_spec, cache_spec] + [pl.BlockSpec(memory_space=pl.ANY)] * len(extra),
            out_specs=(pl.BlockSpec((owners, 1, chunk // owners, dim), lambda h, *_: (0, slot, 0, h)), whole(rows.shape), whole(rows.shape)),
            scratch_shapes=[pltpu.VMEM((chunk, 2 * dim), jnp.float32), pltpu.VMEM((chunk, 128), jnp.float32)],
        ),
        cost_estimate=pl.CostEstimate(flops=4 * heads * chunk * cache_len * dim, bytes_accessed=4 * heads * cache_len * dim, transcendentals=heads * chunk * cache_len),
        input_output_aliases={5: 0} if extra else {},
        name='attend',
    )(prefix_len, slopes, qkv, k_heads, v_heads, *extra)


def prep_kernel(heads, event_ref, k_ref, v_ref, k_copy, v_copy, k_heads, v_heads):
    del event_ref
    n = 256
    per = n // heads
    row = lax.broadcasted_iota(jnp.int32, (n, n), 0)
    pick = (row % per * heads + row // per == lax.broadcasted_iota(jnp.int32, (n, n), 1)).astype(jnp.bfloat16)
    for src, copy, split in ((k_ref, k_copy, k_heads), (v_ref, v_copy, v_heads)):
        copy[...] = src[...]
        for i in range(src.shape[1] // n):
            both = jnp.dot(pick, src[0, pl.ds(i * n, n), :], preferred_element_type=jnp.float32).astype(split.dtype)
            for h in range(heads):
                split[0, h, pl.ds(i * per, per), :] = both[h * per:(h + 1) * per]


def prep_cache(k_cache, v_cache, event, rows=2048):
    batch, length, heads, dim = k_cache.shape
    flat = (batch, length * heads, dim)
    flat_spec = pl.BlockSpec((1, rows, dim), lambda b, i: (b, i, 0))
    split_spec = pl.BlockSpec((1, heads, rows // heads, dim), lambda b, i: (b, 0, i, 0))
    flat_out = jax.ShapeDtypeStruct(flat, k_cache.dtype)
    split_out = jax.ShapeDtypeStruct((batch, heads, length, dim), k_cache.dtype)
    k_copy, v_copy, k_heads, v_heads = pl.pallas_call(
        functools.partial(prep_kernel, heads),
        out_shape=(flat_out, flat_out, split_out, split_out),
        grid=(batch, length * heads // rows),
        in_specs=[pl.BlockSpec(memory_space=pl.ANY), flat_spec, flat_spec],
        out_specs=(flat_spec, flat_spec, split_spec, split_spec),
        cost_estimate=pl.CostEstimate(flops=8 * batch * length * heads * dim * 256, bytes_accessed=12 * batch * length * heads * dim, transcendentals=0),
        name='prep',
    )(event, k_cache.reshape(flat), v_cache.reshape(flat))
    return k_copy.reshape(k_cache.shape), v_copy.reshape(k_cache.shape), k_heads, v_heads


def proj_kernel(early_ref, late_ref, x_ref, w_ref, b_ref, gain_ref, bias_ref, res_ref, norm_ref, owned, wide):
    step = pl.program_id(0)
    blocks, early, tok, part = early_ref.shape
    batch = x_ref.shape[0]

    @pl.when(step == 0)
    def _():
        for b in range(batch):
            src, at = (early_ref, b) if b < early else (late_ref, b - early)
            for t in range(blocks):
                owned[b * tok:(b + 1) * tok, t * part:(t + 1) * part] = src[t, at]

    tile = w_ref.shape[1]
    total = jnp.dot(owned[...], w_ref[...], preferred_element_type=jnp.float32)
    for b in range(batch):
        row = (x_ref[b].astype(jnp.float32) + total[b * tok:(b + 1) * tok] + b_ref[...]).astype(res_ref.dtype)
        res_ref[b] = row
        wide[b * tok:(b + 1) * tok, pl.ds(pl.multiple_of(step * tile, tile), tile)] = row

    @pl.when(step == pl.num_programs(0) - 1)
    def _():
        n = 64

        @pl.loop(0, wide.shape[0] // n)
        def _(i):
            rows = pl.ds(pl.multiple_of(i * n, n), n)
            val = wide[rows, :].astype(jnp.float32)
            centered = val - jnp.mean(val, axis=-1, keepdims=True)
            var = jnp.mean(centered * centered, axis=-1, keepdims=True)
            norm_ref[rows, :] = (centered * lax.rsqrt(var + LN_EPS) * gain_ref[...] + bias_ref[...]).astype(norm_ref.dtype)


def project(early, late, x, w, b, gain, bias, tile=512):
    batch, tok, width = x.shape
    whole = lambda a: pl.BlockSpec(a.shape, lambda j: (0,) * a.ndim)
    row = lambda a: a.astype(jnp.float32)[None]
    gain, bias = row(gain), row(bias)
    bf16 = jnp.bfloat16
    col = pl.BlockSpec((batch, tok, tile), lambda j: (0, 0, j))
    return pl.pallas_call(
        proj_kernel,
        out_shape=(jax.ShapeDtypeStruct(x.shape, bf16), jax.ShapeDtypeStruct((batch * tok, width), bf16)),
        grid=(width // tile,),
        in_specs=[whole(early), whole(late), col, pl.BlockSpec((width, tile), lambda j: (0, j)), pl.BlockSpec((1, tile), lambda j: (0, j)), whole(gain), whole(bias)],
        out_specs=(col, pl.BlockSpec((batch * tok, width), lambda j: (0, 0))),
        scratch_shapes=[pltpu.VMEM((batch * tok, width), bf16), pltpu.VMEM((batch * tok, width), bf16)],
        cost_estimate=pl.CostEstimate(flops=2 * batch * tok * width * width, bytes_accessed=2 * width * width, transcendentals=0),
        name='project',
    )(early, late, x, w, row(b), gain, bias)


def pair_ids(t):
    return {'mate': t + 1 - 2 * (t % 2), 'partner': t + 2 - 4 * (t // 2 % 2)}


def mlp_kernel(a_ref, res_ref, wu_ref, wd_ref, u0, u1, u2, u3, d0, d1, d2, d3, bu_ref, bd_ref, out_ref,
               wu, wd, rows, hid, stage, own, to_mate, to_diag, to_partner, from_mate, from_diag, from_partner, res,
               load_sem, send_sem, recv_sem):
    me = lax.axis_index('tp')
    ids = pair_ids(me)
    quarter = lax.axis_index('dp') % 4
    q_1 = quarter + 1 - 2 * (quarter % 2)
    q_2 = quarter + 2 - 4 * (quarter // 2)
    q_3 = 3 - quarter
    tok, width = own.shape
    blk = hid.shape[0]
    halves = tok // blk
    hid_loc = wu.shape[2]
    tile = 512

    barrier = pltpu.get_barrier_semaphore()
    for who in ('mate', 'partner'):
        pl.semaphore_signal(barrier, inc=1, device_id={'tp': ids[who]}, device_id_type=pl.DeviceIdType.MESH)

    loads = [pltpu.make_async_copy(a_ref, rows.at[0], load_sem.at[0]), pltpu.make_async_copy(wu_ref, wu.at[0], load_sem.at[1])]
    q_rows = u0.shape[0]
    for i, (piece, at) in enumerate(((u0, quarter), (u1, q_1), (u2, q_2), (u3, q_3))):
        loads.append(pltpu.make_async_copy(piece, wu.at[1, pl.ds(pl.multiple_of(at * q_rows, q_rows), q_rows), :], load_sem.at[2 + i]))
    loads.append(pltpu.make_async_copy(wd_ref, wd.at[pl.ds(0, hid_loc), :], load_sem.at[6]))
    q_hid = d0.shape[0]
    for i, (piece, at) in enumerate(((d0, quarter), (d1, q_2), (d2, q_1), (d3, q_3))):
        loads.append(pltpu.make_async_copy(piece, wd.at[pl.ds(pl.multiple_of(hid_loc + at * q_hid, q_hid), q_hid), :], load_sem.at[7 + i]))
    loads.append(pltpu.make_async_copy(res_ref, res, load_sem.at[11]))
    for copy in loads:
        copy.start()

    pl.semaphore_wait(barrier, 2)

    def remote(kind, half, src, dst, who):
        return pltpu.make_async_remote_copy(src_ref=src, dst_ref=dst, send_sem=send_sem.at[kind, half], recv_sem=recv_sem.at[kind, half],
                                            device_id={'tp': ids[who]}, device_id_type=pl.DeviceIdType.MESH)

    def part(half):
        return pl.ds(half * blk, blk)

    rows_mate = [remote(0, h, a_ref.at[part(h)], rows.at[1, part(h)], 'mate') for h in range(halves)]
    rows_partner = [remote(1, h, a_ref.at[part(h)], rows.at[2, part(h)], 'partner') for h in range(halves)]
    rows_diag = [remote(2, h, rows.at[2, part(h)], rows.at[3, part(h)], 'mate') for h in range(halves)]
    sum_mate = [remote(3, h, to_mate.at[part(h)], from_mate.at[part(h)], 'mate') for h in range(halves)]
    sum_diag = [remote(4, h, to_diag.at[part(h)], from_diag.at[part(h)], 'mate') for h in range(halves)]
    sum_partner = [remote(5, h, to_partner.at[part(h)], from_partner.at[part(h)], 'partner') for h in range(halves)]
    for h in range(halves):
        rows_partner[h].start()
    for h in range(halves):
        rows_mate[h].start()
    for copy in loads:
        copy.wait()

    near = 2 * halves

    @pl.loop(0, 2 * near)
    def _(step):
        far = step // near
        k = step % near
        slot = (1 - far) * (k // halves) + far * (3 - k % 2)
        half = (1 - far) * (k % halves) + far * (k // 2)
        for h in range(halves):
            @pl.when(step == halves + h)
            def _(h=h):
                rows_mate[h].wait_recv()

            @pl.when(step == near + 2 * h)
            def _(h=h):
                rows_partner[h].wait_recv()
                rows_diag[h].start()
                rows_diag[h].wait_recv()

        at = pl.ds(pl.multiple_of(half * blk, blk), blk)

        @pl.loop(0, 2 * hid_loc // tile)
        def _(j):
            which = j // (hid_loc // tile)
            off = pl.multiple_of(j % (hid_loc // tile) * tile, tile)
            x = jnp.dot(rows[slot, at, :], wu[which, :, pl.ds(off, tile)], preferred_element_type=jnp.float32)
            x = x + bu_ref[which, :, pl.ds(off, tile)]
            cdf = 0.5 * (1.0 + jnp.tanh(math.sqrt(2.0 / math.pi) * (x + 0.044715 * (x * x * x))))
            hid[:, pl.ds(pl.multiple_of(j * tile, tile), tile)] = (x * cdf).astype(hid.dtype)

        @pl.loop(0, width // tile)
        def _(j):
            cols = pl.ds(pl.multiple_of(j * tile, tile), tile)
            stage[:, cols] = jnp.dot(hid[...], wd[:, cols], preferred_element_type=jnp.float32)

        @pl.when(slot == 0)
        def _():
            own[at, :] = stage[...]

        for h in range(halves):
            @pl.when(step == halves + h)
            def _(h=h):
                to_mate[part(h), :] = stage[...].astype(to_mate.dtype)
                sum_mate[h].start()

            @pl.when(step == near + 2 * h)
            def _(h=h):
                to_diag[part(h), :] = stage[...].astype(to_diag.dtype)
                sum_diag[h].start()

            @pl.when(step == near + 2 * h + 1)
            def _(h=h):
                sum_diag[h].wait_recv()
                to_partner[part(h), :] = (stage[...] + from_diag[part(h), :].astype(jnp.float32)).astype(to_partner.dtype)
                sum_partner[h].start()

    for h in range(halves):
        sum_mate[h].wait_recv()
        sum_partner[h].wait_recv()
        total = own[part(h), :] + from_mate[part(h), :].astype(jnp.float32) + from_partner[part(h), :].astype(jnp.float32)
        out_ref[part(h), :] = (res[part(h), :].astype(jnp.float32) + total + bd_ref[...]).astype(out_ref.dtype)
    for copies in (rows_mate, rows_partner, rows_diag, sum_mate, sum_diag, sum_partner):
        for copy in copies:
            copy.wait_send()


def mlp(a, res, w_up, w_down, up_parts, down_parts, bias_up, bias_down, blk=256):
    tok, width = a.shape
    hid_loc = w_up.shape[1]
    any_spec = pl.BlockSpec(memory_space=pl.ANY)
    vmem = pl.BlockSpec(memory_space=pltpu.VMEM)
    bf16, f32 = jnp.bfloat16, jnp.float32
    return pl.pallas_call(
        mlp_kernel,
        out_shape=jax.ShapeDtypeStruct((tok, width), bf16),
        in_specs=[any_spec] * 12 + [vmem, vmem],
        out_specs=vmem,
        scratch_shapes=[
            pltpu.VMEM((2, width, hid_loc), bf16),
            pltpu.VMEM((2 * hid_loc, width), bf16),
            pltpu.VMEM((4, tok, width), bf16),
            pltpu.VMEM((blk, 2 * hid_loc), bf16),
            pltpu.VMEM((blk, width), f32),
            pltpu.VMEM((tok, width), f32),
        ] + [pltpu.VMEM((tok, width), bf16)] * 7 + [
            pltpu.SemaphoreType.DMA((12,)),
            pltpu.SemaphoreType.DMA((6, tok // blk)),
            pltpu.SemaphoreType.DMA((6, tok // blk)),
        ],
        compiler_params=pltpu.CompilerParams(collective_id=0, has_side_effects=True, vmem_limit_bytes=62 << 20),
        cost_estimate=pl.CostEstimate(flops=32 * tok * width * hid_loc, bytes_accessed=8 * width * hid_loc, transcendentals=0),
        name='mlp',
    )(a, res, w_up, w_down, *up_parts, *down_parts, bias_up, bias_down)


def after(value, *events):
    return lax.optimization_barrier((value,) + events)[0]


def solution(mesh):
    tp_size = mesh.shape['tp']

    def local_layer(x_local, prefix_len, k_cache, v_cache, ln1_gain, ln1_bias, w_qkv, b_qkv, w_out, b_out, ln2_gain, ln2_bias, w_up, b_up, w_down, b_down):
        batch_n, tok_loc, width = x_local.shape
        heads_loc, head_dim = k_cache.shape[2], k_cache.shape[3]
        chunk_len = tok_loc * tp_size
        head_ids = lax.axis_index('tp') * heads_loc + jnp.arange(heads_loc)
        slopes = jnp.exp2(-8.0 * (head_ids + 1).astype(jnp.float32) / (heads_loc * tp_size))
        mirror = [(t, tp_size - 2 - 2 * (t // 2) + t % 2) for t in range(tp_size)]
        flips = [[(d, d ^ bit) for d in range(mesh.shape['dp'])] for bit in (1, 2)]
        quarter = lax.axis_index('dp') % 4
        b_up_far = lax.ppermute(b_up, 'tp', mirror)
        bias_up = jnp.stack([b_up, b_up_far])[:, None].astype(jnp.float32)
        normed = layer_norm(x_local, ln1_gain, ln1_bias)
        gathers = []
        for seq in range(batch_n):
            gathers.append(lax.all_gather(normed[seq], 'tp', axis=0, tiled=True))
        k_upd, v_upd, k_heads, v_heads = prep_cache(k_cache, v_cache, normed)

        q_up, q_down = w_up.shape[0] // 4, w_down.shape[0] // 4
        u_0 = lax.ppermute(lax.dynamic_slice_in_dim(w_up, quarter * q_up, q_up), 'tp', mirror)
        d_0 = lax.ppermute(lax.dynamic_slice_in_dim(w_down, quarter * q_down, q_down), 'tp', mirror)
        u_1 = lax.ppermute(u_0, 'dp', flips[0])
        d_1 = lax.ppermute(d_0, 'dp', flips[1])
        u_2 = lax.ppermute(u_0, 'dp', flips[1])
        d_2 = lax.ppermute(d_0, 'dp', flips[0])
        u_3 = lax.ppermute(u_1, 'dp', flips[1])
        d_3 = lax.ppermute(d_1, 'dp', flips[0])
        up_parts, down_parts = (u_0, u_1, u_2, u_3), (d_0, d_1, d_2, d_3)
        rows_new, exchanged = [], []
        zero = jnp.zeros((), jnp.int32)
        early, context = batch_n - 1, None
        for seq in range(batch_n):
            gathered = gathers[seq] if seq == 0 else after(gathers[seq], rows_new[-1][0])
            qkv = (jnp.dot(gathered, w_qkv, preferred_element_type=jnp.float32) + b_qkv.astype(jnp.float32)).astype(jnp.bfloat16)
            where = dict(slots=early, slot=seq, buffer=context) if seq < early else {}
            context, k_new, v_new = attend(seq, prefix_len, slopes, qkv, k_heads, v_heads, owners=tp_size, **where)
            rows_new.append((k_new, v_new))
            if seq >= early - 1:
                exchanged.append(lax.all_to_all(context, 'tp', 0, 0))
        for seq, (k_new, v_new) in enumerate(rows_new):
            at = (jnp.int32(seq), prefix_len[seq], zero, zero)
            new_shape = (1, chunk_len, heads_loc, head_dim)
            k_upd = lax.dynamic_update_slice(k_upd, k_new.reshape(new_shape), at)
            v_upd = lax.dynamic_update_slice(v_upd, v_new.reshape(new_shape), at)
        w_out_all = lax.all_gather(w_out, 'tp', axis=0, tiled=True)
        residual, normed2 = project(*exchanged, x_local, w_out_all, b_out, ln2_gain, ln2_bias)
        tok = batch_n * tok_loc
        x_out = mlp(normed2, residual.reshape(tok, width), w_up, w_down, up_parts, down_parts, bias_up, b_down.astype(jnp.float32)[None])
        return x_out.reshape(batch_n, tok_loc, width), k_upd, v_upd

    tok_spec = P('dp', 'tp', None)
    cache_spec = P('dp', None, 'tp', None)
    replicated = P()
    in_specs = (tok_spec, P('dp'), cache_spec, cache_spec, replicated, replicated, P(None, 'tp'), P('tp'), P('tp', None), replicated, replicated, replicated, P(None, 'tp'), P('tp'), P('tp', None), replicated)
    return jax.shard_map(local_layer, mesh=mesh, in_specs=in_specs, out_specs=(tok_spec, cache_spec, cache_spec), check_vma=False)
```

time: 692 us -> 404 us (0.58)
  waiting for transfers between devices: 308 us -> 67.6 us
  Pallas kernels: 0 us -> 207 us
  matrix products: 223 us -> 32.1 us
  other arithmetic: 111 us -> 10.1 us
  starting transfers between devices: 0.44 us -> 22.8 us
  blocking collectives: 0 us -> 18.4 us
  local copies, waits for them, and re-layouts: 34.3 us -> 20 us
  between operations: 14 us -> 21.8 us
    pallas_call x0 -> x7, Pallas kernels: none -> 207 us  [the longest x1 97.5 us: mlp(): pl.pallas_call(mlp_kernel, out_shape=jax.ShapeDtypeStruct((tok, width), b...]
    reduce_scatter x2 -> x0, waiting for transfers between devices: 176 us -> none  [the longest x1 87.9 us: local_layer(): lax.psum_scatter(attn_part, 'tp', scatter_dimension=1, tiled=True)]
    all_gather x2 -> x5, waiting for transfers between devices: 132 us -> 0.03 us  [the longest x4 0.03 us: local_layer(): gathers.append(lax.all_gather(normed[seq], 'tp', axis=0, tiled=True))]
    sub x1 -> x0, matrix products: 105 us -> none  [attend(): attn_probs = jax.nn.softmax(scores, axis=-1).astype(jnp.bfloat16)]
    dot_general x5 -> x4, matrix products: 118 us -> 32.1 us  [local_layer(): jnp.dot(gathered, w_qkv, preferred_element_type=jnp.float32)]
    ppermute x0 -> x9, waiting for transfers between devices: none -> 65.4 us  [the longest x1 29.5 us: local_layer(): lax.ppermute(lax.dynamic_slice_in_dim(w_down, quarter * q_down, q_down),...]
    scatter x17 -> x0, other arithmetic: 60.9 us -> none
    convert_element_type x5 -> x1, other arithmetic: 25.9 us -> 0.61 us  [local_layer(): bias_up = jnp.stack([b_up, b_up_far])[:, None].astype(jnp.float32)]
  transfers between devices with their start and end apart: 4 -> 15, of which waited for: 4 -> 5; matrix products, arithmetic and copies ran while one was open for 5% -> 12% of each run, Pallas kernels for 0% -> 27%
where the time goes in v1:
time: 404 us; the launch traced here: 400 us
  Pallas kernels  207 us (51%)
  waiting for transfers between devices  67.6 us (17%)
  matrix products  32.1 us (8%)
  starting transfers between devices  22.8 us (6%)
  between operations  21.8 us (5%)
  local copies, waits for them, and re-layouts  20 us (5%)
  blocking collectives  18.4 us (5%)
  other arithmetic  10.1 us (2%)
    pallas_call x1, Pallas kernels, mlp(): pl.pallas_call(mlp_kernel, out_shape=jax.ShapeDtypeStruct((tok, width), b...  97.5 us
    pallas_call x4, Pallas kernels, attend(): pl.pallas_call(functools.partial(attn_kernel, seq, q_blk, k_blk), out_sha...  72.9 us
    dot_general x4, matrix products, local_layer(): jnp.dot(gathered, w_qkv, preferred_element_type=jnp.float32)  32.1 us
    ppermute x1, waiting for transfers between devices, local_layer(): lax.ppermute(lax.dynamic_slice_in_dim(w_down, quarter * q_down, q_down),...  29.5 us
    pallas_call x1, Pallas kernels, prep_cache(): pl.pallas_call(functools.partial(prep_kernel, heads), out_shape=(flat_out...  23.6 us
    ppermute x1, waiting for transfers between devices, local_layer(): u_3 = lax.ppermute(u_1, 'dp', flips[1])  20 us
    all_to_all x1, blocking collectives, local_layer(): exchanged.append(lax.all_to_all(context, 'tp', 0, 0))  18.4 us
    ppermute x1, waiting for transfers between devices, local_layer(): lax.ppermute(lax.dynamic_slice_in_dim(w_up, quarter * q_up, q_up), 'tp',...  13.2 us
  transfers between devices with their start and end apart: 15, of which 5 were waited for; matrix products, arithmetic and copies ran while one was open for 12% of the time, Pallas kernels for 27%

profile of v1, /device:TPU:81, one launch (start us, length us, event | category | flops | bytes accessed | tf_op | source)
XLA Modules:
  0.0 399.7 jit_solution(11168340333228859965)
XLA Ops:
  10.7 2.3 fusion.2
  20.9 3.8 collective-permute-start
  26.7 23.6 %prep.1 = (bf16[4,8192,128]{2,1,0:T(8,128)(2,1)}, bf16[4,8192,128]{2,1,0:T(8,128)(2,1)}, bf16[4,2,4096,128]{3,2,1,0:T(8,128)(2,1)}, bf16[4,2,4096,128]{3,2,1,0:T(8,128)(2,1)}) custom-call(bf16[4,128,2048]{2,1,0:T(8,128)(2,1)} %copy-done.1, bf16[4,8192,128]{2,1,0:T(8,128)(2,1)} %bitcast.50, bf16[4,8192,128]{2,1,0:T(8,128)(2,1)} %bitcast.51), custom_call_target="tpu_custom_call" | custom-call | flops 8589934592 | bytes 50331648 | tf_op jit(solution)/shard_map/prep/pallas_call | solution.py:140
  50.3 13.2 %collective-permute-done.u0 = bf16[512,1024]{1,0:T(8,128)(2,1)} collective-permute-done((bf16[512,1024]{1,0:T(8,128)(2,1)S(1)}, bf16[512,1024]{1,0:T(8,128)(2,1)}, u32[]{:S(2)}, u32[]{:S(2)}) %collective-permute-start) | collective-permute-done | bytes 1048608 | tf_op jit(solution)/shard_map/ppermute | solution.py:380
  63.4 3.6 collective-permute-start.1
  67.0 29.5 %collective-permute-done.4.d0 = bf16[256,2048]{1,0:T(8,128)(2,1)} collective-permute-done((bf16[256,2048]{1,0:T(8,128)(2,1)S(1)}, bf16[256,2048]{1,0:T(8,128)(2,1)}, u32[]{:S(2)}, u32[]{:S(2)}) %collective-permute-start.4) | collective-permute-done | bytes 1048608 | tf_op jit(solution)/shard_map/ppermute | solution.py:381
  96.5 2.2 collective-permute-start.5
  98.7 7.9 %add_convert_fusion.3.qkv_ref = bf16[1024,768]{1,0:T(8,128)(2,1)} fusion(bf16[2048,768]{1,0:T(8,128)(2,1)} %param.22, bf16[1,1024,2048]{2,1,0:T(8,128)(2,1)} %all-gather.16.cloned.1.call-done, f32[768]{0:T(1024)S(1)} %convert_element_type.45), kind=kOutput, calls=%fused_computation.13 | convolution fusion | flops 3222798336 | bytes 8915968 | tf_op jit(solution)/shard_map/dot_general | solution.py:394
  106.6 21.1 %attend.4 = (bf16[8,3,128,256]{3,2,1,0:T(8,128)(2,1)}, bf16[2048,128]{1,0:T(8,128)(2,1)}, bf16[2048,128]{1,0:T(8,128)(2,1)}) custom-call(s32[4]{0:T(128)} %prefix_ref.7, f32[2]{0:T(128)} %multiply_exponential_fusion.slope_ref, bf16[1024,768]{1,0:T(8,128)(2,1)} %add_convert_fusion.3.qkv_ref, bf16[4,2,4096,128]{3,2,1,0:T(8,128)(2,1)} %get-tuple-element.24.k_ref, ...), custom_call_target="tpu_custom_call" | custom-call | flops 4294967296 | bytes 4194304 | tf_op jit(solution)/shard_map/attend/pallas_call | solution.py:103
  127.8 7.9 %add_convert_fusion.2.qkv_ref = bf16[1024,768]{1,0:T(8,128)(2,1)} fusion(bf16[1024,2048]{1,0:T(8,128)(2,1)} %bitcast.56, bf16[2048,768]{1,0:T(8,128)(2,1)} %param.22, f32[768]{0:T(1024)S(1)} %convert_element_type.45), kind=kOutput, calls=%fused_computation.12 | convolution fusion | flops 3222798336 | bytes 8915968 | tf_op jit(solution)/shard_map/dot_general | solution.py:394
  135.6 13.4 %attend.5 = (bf16[8,3,128,256]{3,2,1,0:T(8,128)(2,1)}, bf16[2048,128]{1,0:T(8,128)(2,1)}, bf16[2048,128]{1,0:T(8,128)(2,1)}) custom-call(s32[4]{0:T(128)} %prefix_ref.7, f32[2]{0:T(128)} %multiply_exponential_fusion.slope_ref, bf16[1024,768]{1,0:T(8,128)(2,1)} %add_convert_fusion.2.qkv_ref, ...), custom_call_target="tpu_custom_call", output_to_operand_aliasing={{0}: (5, {})} | custom-call | flops 4294967296 | bytes 4194304 | tf_op jit(solution)/shard_map/attend/pallas_call | solution.py:103
  149.1 7.7 %add_convert_fusion.1.qkv_ref = bf16[1024,768]{1,0:T(8,128)(2,1)} fusion(bf16[1024,2048]{1,0:T(8,128)(2,1)} %bitcast.55, bf16[2048,768]{1,0:T(8,128)(2,1)} %param.22, f32[768]{0:T(1024)S(1)} %convert_element_type.45), kind=kOutput, calls=%fused_computation.11 | convolution fusion | flops 3222798336 | bytes 8915968 | tf_op jit(solution)/shard_map/dot_general | solution.py:394
  156.8 21.2 %attend.6 = (bf16[8,3,128,256]{3,2,1,0:T(8,128)(2,1)}, bf16[2048,128]{1,0:T(8,128)(2,1)}, bf16[2048,128]{1,0:T(8,128)(2,1)}) custom-call(s32[4]{0:T(128)} %prefix_ref.7, f32[2]{0:T(128)} %multiply_exponential_fusion.slope_ref, bf16[1024,768]{1,0:T(8,128)(2,1)} %add_convert_fusion.1.qkv_ref, ...), custom_call_target="tpu_custom_call", output_to_operand_aliasing={{0}: (5, {})} | custom-call | flops 4294967296 | bytes 4194304 | tf_op jit(solution)/shard_map/attend/pallas_call | solution.py:103
  178.0 8.7 %add_convert_fusion.qkv_ref = bf16[1024,768]{1,0:T(8,128)(2,1)} fusion(bf16[1024,2048]{1,0:T(8,128)(2,1)} %bitcast.54, bf16[2048,768]{1,0:T(8,128)(2,1)} %param.22, f32[768]{0:T(1024)S(1)} %convert_element_type.45), kind=kOutput, calls=%fused_computation.10 | convolution fusion | flops 3222798336 | bytes 8915968 | tf_op jit(solution)/shard_map/dot_general | solution.py:394
  186.7 17.2 %attend.7 = (bf16[8,1,128,256]{3,2,1,0:T(8,128)(2,1)}, bf16[2048,128]{1,0:T(8,128)(2,1)}, bf16[2048,128]{1,0:T(8,128)(2,1)}) custom-call(s32[4]{0:T(128)} %prefix_ref.7, f32[2]{0:T(128)} %multiply_exponential_fusion.slope_ref, bf16[1024,768]{1,0:T(8,128)(2,1)} %add_convert_fusion.qkv_ref, bf16[4,2,4096,128]{3,2,1,0:T(8,128)(2,1)} %get-tuple-element.24.k_ref, ...), custom_call_target="tpu_custom_call" | custom-call | flops 4294967296 | bytes 4194304 | tf_op jit(solution)/shard_map/attend/pallas_call | solution.py:103
  203.9 18.4 %all_to_all.10.late_ref = bf16[8,1,128,256]{3,2,1,0:T(8,128)(2,1)} all-to-all(bf16[8,1,128,256]{3,2,1,0:T(8,128)(2,1)} %get-tuple-element.35), channel_id=1, replica_groups=mesh['dp'=4,'tp'=8] {'tp'}, dimensions={0} | all-to-all | bytes 1048576 | tf_op jit(solution)/shard_map/all_to_all | solution.py:399
  222.3 4.7 %all-to-all-start = ((bf16[8,3,128,256]{3,2,1,0:T(8,128)(2,1)}), bf16[8,3,128,256]{3,2,1,0:T(8,128)(2,1)S(1)}, u32[]{:S(2)}, u32[]{:S(2)}) async-start(bf16[8,3,128,256]{3,2,1,0:T(8,128)(2,1)} %get-tuple-element.32), calls=%async_computation | async-start | bytes 3145728 | tf_op jit(solution)/shard_map/all_to_all | solution.py:399
  227.0 2.8 collective-permute-start.8
  243.0 3.1 collective-permute-start.2
  249.5 2.2 constant_dynamic-update-slice_fusion.6
  258.6 12.8 %project.1 = (bf16[4,128,2048]{2,1,0:T(8,128)(2,1)}, bf16[512,2048]{1,0:T(8,128)(2,1)}) custom-call(bf16[8,3,128,256]{3,2,1,0:T(8,128)(2,1)} %copy-done.2, bf16[8,1,128,256]{3,2,1,0:T(8,128)(2,1)} %all_to_all.10.late_ref, bf16[4,128,2048]{2,1,0:T(8,128)(2,1)} %x_ref.1, bf16[2048,2048]{1,0:T(8,128)(2,1)} %all-gather.10.cloned.1.call-done.w_ref, ...), custom_call_target="tpu_custom_call" | custom-call | flops 4294967296 | bytes 8388608 | tf_op jit(solution)/shard_map/project/pallas_call | solution.py:191
  271.5 20.0 %collective-permute-done.3.u3 = bf16[512,1024]{1,0:T(8,128)(2,1)} collective-permute-done((bf16[512,1024]{1,0:T(8,128)(2,1)}, bf16[512,1024]{1,0:T(8,128)(2,1)}, u32[]{:S(2)}, u32[]{:S(2)}) %collective-permute-start.3) | collective-permute-done | bytes 1048608 | tf_op jit(solution)/shard_map/ppermute | solution.py:386
  292.3 97.5 %mlp.1 = bf16[512,2048]{1,0:T(8,128)(2,1)} custom-call(bf16[512,2048]{1,0:T(8,128)(2,1)} %get-tuple-element.36.a_ref, bf16[512,2048]{1,0:T(8,128)(2,1)} %bitcast.57, bf16[2048,1024]{1,0:T(8,128)(2,1)} %wu_ref.1, bf16[1024,2048]{1,0:T(8,128)(2,1)} %wd_ref.1, bf16[512,1024]{1,0:T(8,128)(2,1)} %collective-permute-done.u0, ...), custom_call_target="tpu_custom_call" | custom-call | flops 34359738368 | bytes 16777216 | tf_op jit(solution)/shard_map/mlp/pallas_call | solution.py:332
  389.8 3.2 copy.32
  (85 shorter events, 30.1 us)
Async XLA Ops:
  7.2 91.5 %all-gather.16.cloned.1.call-start = ((), (), s32[]{:S(2)}) async-start(), calls=%async_computation.5 | async-start | bytes 4718592 | tf_op jit(solution)/shard_map/all_gather | solution.py:376
  16.7 111.1 %all-gather.14.cloned.1.call-start = ((), (), s32[]{:S(2)}) async-start(), calls=%async_computation.4 | async-start | bytes 4718592 | tf_op jit(solution)/shard_map/all_gather | solution.py:376
  17.5 131.6 %all-gather.12.cloned.1.call-start = ((), (), s32[]{:S(2)}) async-start(), calls=%async_computation.3 | async-start | bytes 4718592 | tf_op jit(solution)/shard_map/all_gather | solution.py:376
  18.3 159.7 %all-gather.18.cloned.1.call-start = ((), (), s32[]{:S(2)}) async-start(), calls=%async_computation.6 | async-start | bytes 4718592 | tf_op jit(solution)/shard_map/all_gather | solution.py:376
  18.9 238.6 %all-gather.10.cloned.1.call-start = ((), (), s32[]{:S(2)}) async-start(), calls=%async_computation.2 | async-start | bytes 9437184 | tf_op jit(solution)/shard_map/all_gather | solution.py:405
  20.9 42.6 %collective-permute-start = (bf16[512,1024]{1,0:T(8,128)(2,1)S(1)}, bf16[512,1024]{1,0:T(8,128)(2,1)}, u32[]{:S(2)}, u32[]{:S(2)}) collective-permute-start(bf16[512,1024]{1,0:T(8,128)(2,1)S(1)} %constant_dynamic-slice_fusion.1), channel_id=1, source_target_pairs={{0,6},{1,7},{2,4},{3,5},{4,2},{5,3},{6,0},{7,1},{8,14},{9,15},{10,... | collective-permute-start | bytes 3145736 | tf_op jit(solution)/shard_map/ppermute | solution.py:380
  26.0 70.5 %collective-permute-start.4 = (bf16[256,2048]{1,0:T(8,128)(2,1)S(1)}, bf16[256,2048]{1,0:T(8,128)(2,1)}, u32[]{:S(2)}, u32[]{:S(2)}) collective-permute-start(bf16[256,2048]{1,0:T(8,128)(2,1)S(1)} %constant_dynamic-slice_fusion), channel_id=1, source_target_pairs={{0,6},{1,7},{2,4},{3,5},{4,2},{5,3},{6,0},{7,1},{8,14},{9,15},{10,... | collective-permute-start | bytes 3145736 | tf_op jit(solution)/shard_map/ppermute | solution.py:381
  63.4 182.8 %collective-permute-start.1 = (bf16[512,1024]{1,0:T(8,128)(2,1)}, bf16[512,1024]{1,0:T(8,128)(2,1)}, u32[]{:S(2)}, u32[]{:S(2)}) collective-permute-start(bf16[512,1024]{1,0:T(8,128)(2,1)} %collective-permute-done.u0), channel_id=1, source_target_pairs={{0,8},{8,0},{16,24},{24,16},{1,9},{9,1},{17,25},{25,17},{2,10},{10... | collective-permute-start | bytes 3145736 | tf_op jit(solution)/shard_map/ppermute | solution.py:382
  96.5 151.2 %collective-permute-start.5 = (bf16[256,2048]{1,0:T(8,128)(2,1)}, bf16[256,2048]{1,0:T(8,128)(2,1)}, u32[]{:S(2)}, u32[]{:S(2)}) collective-permute-start(bf16[256,2048]{1,0:T(8,128)(2,1)} %collective-permute-done.4.d0), channel_id=1, source_target_pairs={{0,16},{8,24},{16,0},{24,8},{1,17},{9,25},{17,1},{25,9},{2,18},{10... | collective-permute-start | bytes 3145736 | tf_op jit(solution)/shard_map/ppermute | solution.py:383
  203.8 23.2 %copy-start.16 = (bf16[1024]{0:T(1024)(128)(2,1)S(1)}, bf16[1024]{0:T(1024)(128)(2,1)}, u32[]{:S(2)}) copy-start(bf16[1024]{0:T(1024)(128)(2,1)} %param.29) | copy-start | bytes 6148
  203.8 26.0 %copy-start.10 = (s32[4]{0:T(128)S(1)}, s32[4]{0:T(128)}, u32[]{:S(2)}) copy-start(s32[4]{0:T(128)} %prefix_ref.7) | copy-start | bytes 52
  203.8 31.7 %copy-start.11 = (bf16[2048]{0:T(1024)(128)(2,1)S(1)}, bf16[2048]{0:T(1024)(128)(2,1)}, u32[]{:S(2)}) copy-start(bf16[2048]{0:T(1024)(128)(2,1)} %param.25) | copy-start | bytes 12292
  203.9 32.3 %copy-start.12 = (bf16[2048]{0:T(1024)(128)(2,1)S(1)}, bf16[2048]{0:T(1024)(128)(2,1)}, u32[]{:S(2)}) copy-start(bf16[2048]{0:T(1024)(128)(2,1)} %param.26) | copy-start | bytes 12292
  203.9 32.9 %copy-start.13 = (bf16[2048]{0:T(1024)(128)(2,1)S(1)}, bf16[2048]{0:T(1024)(128)(2,1)}, u32[]{:S(2)}) copy-start(bf16[2048]{0:T(1024)(128)(2,1)} %param.27) | copy-start | bytes 12292
  203.9 33.5 %copy-start.14 = (bf16[2048]{0:T(1024)(128)(2,1)S(1)}, bf16[2048]{0:T(1024)(128)(2,1)}, u32[]{:S(2)}) copy-start(bf16[2048]{0:T(1024)(128)(2,1)} %param.31) | copy-start | bytes 12292
  203.9 43.9 %copy-start.3 = (bf16[2048,128]{1,0:T(8,128)(2,1)S(1)}, bf16[2048,128]{1,0:T(8,128)(2,1)}, u32[]{:S(2)}) copy-start(bf16[2048,128]{1,0:T(8,128)(2,1)} %get-tuple-element.26) | copy-start | bytes 1572868
  203.9 43.9 %copy-start.4 = (bf16[2048,128]{1,0:T(8,128)(2,1)S(1)}, bf16[2048,128]{1,0:T(8,128)(2,1)}, u32[]{:S(2)}) copy-start(bf16[2048,128]{1,0:T(8,128)(2,1)} %get-tuple-element.41) | copy-start | bytes 1572868
  203.9 47.8 %copy-start.5 = (bf16[2048,128]{1,0:T(8,128)(2,1)S(1)}, bf16[2048,128]{1,0:T(8,128)(2,1)}, u32[]{:S(2)}) copy-start(bf16[2048,128]{1,0:T(8,128)(2,1)} %get-tuple-element.42) | copy-start | bytes 1572868
  222.3 35.2 %all-to-all-start = ((bf16[8,3,128,256]{3,2,1,0:T(8,128)(2,1)}), bf16[8,3,128,256]{3,2,1,0:T(8,128)(2,1)S(1)}, u32[]{:S(2)}, u32[]{:S(2)}) async-start(bf16[8,3,128,256]{3,2,1,0:T(8,128)(2,1)} %get-tuple-element.32), calls=%async_computation | async-start | bytes 3145728 | tf_op jit(solution)/shard_map/all_to_all | solution.py:399
  227.0 15.4 %collective-permute-start.8 = (bf16[1024]{0:T(1024)(128)(2,1)S(1)}, bf16[1024]{0:T(1024)(128)(2,1)S(1)}, u32[]{:S(2)}, u32[]{:S(2)}) collective-permute-start(bf16[1024]{0:T(1024)(128)(2,1)S(1)} %copy-done.16), channel_id=1, source_target_pairs={{0,6},{1,7},{2,4},{3,5},{4,2},{5,3},{6,0},{7,1},{8,14},{9,15},{10,... | collective-permute-start | bytes 6152 | tf_op jit(solution)/shard_map/ppermute | solution.py:371
  243.0 28.4 %collective-permute-start.2 = (bf16[512,1024]{1,0:T(8,128)(2,1)}, bf16[512,1024]{1,0:T(8,128)(2,1)}, u32[]{:S(2)}, u32[]{:S(2)}) collective-permute-start(bf16[512,1024]{1,0:T(8,128)(2,1)} %collective-permute-done.u0), channel_id=1, source_target_pairs={{0,16},{8,24},{16,0},{24,8},{1,17},{9,25},{17,1},{25,9},{2,18},{10... | collective-permute-start | bytes 3145736 | tf_op jit(solution)/shard_map/ppermute | solution.py:384
  246.1 25.3 %collective-permute-start.6 = (bf16[256,2048]{1,0:T(8,128)(2,1)}, bf16[256,2048]{1,0:T(8,128)(2,1)}, u32[]{:S(2)}, u32[]{:S(2)}) collective-permute-start(bf16[256,2048]{1,0:T(8,128)(2,1)} %collective-permute-done.4.d0), channel_id=1, source_target_pairs={{0,8},{8,0},{16,24},{24,16},{1,9},{9,1},{17,25},{25,17},{2,10},{10... | collective-permute-start | bytes 3145736 | tf_op jit(solution)/shard_map/ppermute | solution.py:385
  246.3 45.1 %collective-permute-start.3 = (bf16[512,1024]{1,0:T(8,128)(2,1)}, bf16[512,1024]{1,0:T(8,128)(2,1)}, u32[]{:S(2)}, u32[]{:S(2)}) collective-permute-start(bf16[512,1024]{1,0:T(8,128)(2,1)} %collective-permute-done.1.u1), channel_id=1, source_target_pairs={{0,16},{8,24},{16,0},{24,8},{1,17},{9,25},{17,1},{25,9},{2,18},{10... | collective-permute-start | bytes 3145736 | tf_op jit(solution)/shard_map/ppermute | solution.py:386
  247.8 44.6 %collective-permute-start.7 = (bf16[256,2048]{1,0:T(8,128)(2,1)}, bf16[256,2048]{1,0:T(8,128)(2,1)}, u32[]{:S(2)}, u32[]{:S(2)}) collective-permute-start(bf16[256,2048]{1,0:T(8,128)(2,1)} %collective-permute-done.5.d1), channel_id=1, source_target_pairs={{0,8},{8,0},{16,24},{24,16},{1,9},{9,1},{17,25},{25,17},{2,10},{10... | collective-permute-start | bytes 3145736 | tf_op jit(solution)/shard_map/ppermute | solution.py:387
  (8 other events, 74.0 us)
Sparse Core Ops, SparseCore 0:
  16.8 50.4 all-gather.15
  68.9 37.4 all-gather.13
  108.0 31.8 all-gather.11
  141.4 28.8 all-gather.17
  171.8 47.4 all-gather.9
